TPU v7x, 32 devices: a whole 2x2x4 slice. The times are simulated.
32 devices in a mesh: tm: 2 (over x), src: 16 (over z, y, core).
Axes of the slice: x: 2, y: 2, z: 4, core: 2. Of those that a mesh axis runs over, the one named last changes fastest.
Arguments:
- design: float32 [16, 524288], P(None, ('tm', 'src')), may hold values from -2 to 2
- unit_index: int32 [524288], P(('tm', 'src')), may hold values from 0 to 255, as said below
- residual: float32 [524288], P(('tm', 'src')), may hold values from -6 to 6
- weight: float32 [524288], P(('tm', 'src')), may hold values from 0.25 to 4
- obs_count: int32 [32], P(('tm', 'src')), may hold values from 1 to 16384, as said below
- damping: float32 [256], P(('tm', 'src')), may hold values from 1 to 10
Outputs:
- solution: float32 [16, 256], P(None, ('tm', 'src'))
- misfit: float32 [], replicated
Inputs may be any that keep to these rules, and one draw needn't show every extreme that they name: `unit_index`: an observation on a device of tm index g names a unit in [g * 128, (g + 1) * 128). `obs_count`: some device has all 16384 slots live.
All inputs are finite; a program needn't handle non-finite values.
Results may differ from a plain program's by a relative error of at most 0.0003.
Values sent between devices are 32-bit elements; how exact they have to be, the bound alone decides.
A program may use at most 64 MiB of HBM per device.

v0:
```python
import jax
import jax.numpy as jnp
from jax import lax
from jax.sharding import PartitionSpec as P


def make_reader(stacked):

    def reader(row, column):
        return stacked[row * 16 + column]

    return reader


def block_solve(reader, rhs, damping):
    lower = {}
    for j in range(16):
        running = reader(j, j) + damping
        for k in range(j):
            running = running - lower[j, k] * lower[j, k]
        diag_term = jnp.sqrt(running)
        lower[j, j] = diag_term
        for i in range(j + 1, 16):
            running = reader(i, j)
            for k in range(j):
                running = running - lower[i, k] * lower[j, k]
            lower[i, j] = running / diag_term
    forward = []
    for i in range(16):
        running = rhs[i]
        for k in range(i):
            running = running - lower[i, k] * forward[k]
        forward.append(running / lower[i, i])
    backward = [None] * 16
    for i in range(15, -1, -1):
        running = forward[i]
        for k in range(i + 1, 16):
            running = running - lower[k, i] * backward[k]
        backward[i] = running / lower[i, i]
    return jnp.stack(backward)


def quadratic_terms(reader, rhs, solution_own):
    quadratic = jnp.zeros((), jnp.float32)
    for i in range(16):
        applied = jnp.zeros_like(solution_own[0])
        for j in range(16):
            applied = applied + reader(max(i, j), min(i, j)) * solution_own[j]
        quadratic = quadratic + jnp.sum(solution_own[i] * applied)
    return quadratic - 2.0 * jnp.sum(solution_own * rhs)


def on_device(design, unit_index, residual, weight, obs_count, damping):
    n_source = lax.axis_size("src")
    own_units = damping.shape[0]
    units_group = own_units * n_source
    slots = design.shape[1]
    local_unit = unit_index - lax.axis_index("tm") * units_group
    weights_on = jnp.where(
        jnp.arange(slots, dtype=jnp.int32) < obs_count[0], weight, jnp.zeros_like(weight)
    )
    block_rows = 1024
    turns = slots // block_rows
    pair_count = 256

    def pair_rows(rows):
        return (rows[:, None, :] * rows[None, :, :]).reshape(256, rows.shape[1])

    unit_range = jnp.arange(units_group, dtype=jnp.int32)

    def accumulate(step, partial_value):
        begin = step * block_rows
        rows = lax.dynamic_slice_in_dim(design, begin, block_rows, 1)
        units_of = lax.dynamic_slice_in_dim(local_unit, begin, block_rows, 0)
        resid = lax.dynamic_slice_in_dim(residual, begin, block_rows, 0)
        weights_blk = lax.dynamic_slice_in_dim(weights_on, begin, block_rows, 0)
        stacked = jnp.concatenate(
            [pair_rows(rows) * weights_blk, rows * (weights_blk * resid)], axis=0
        )
        one_hot = (units_of[:, None] == unit_range[None, :]).astype(jnp.float32)
        return partial_value + jnp.dot(
            stacked, one_hot, precision=lax.Precision.HIGHEST, preferred_element_type=jnp.float32
        )

    start = jnp.zeros((pair_count + 16, units_group), jnp.float32)
    partial_value = lax.fori_loop(0, turns, accumulate, start)
    own_part = lax.psum_scatter(partial_value, "src", scatter_dimension=1, tiled=True)
    solution_own = block_solve(make_reader(own_part), own_part[pair_count:], damping)
    unit_terms = quadratic_terms(make_reader(own_part), own_part[pair_count:], solution_own)
    before = jnp.sum(weights_on * residual * residual)
    chi_total, weight_total = lax.psum((before + unit_terms, jnp.sum(weights_on)), ("tm", "src"))
    return (solution_own, chi_total / weight_total)


def solution(mesh):
    placed = (
        P(None, ("tm", "src")),
        P(("tm", "src")),
        P(("tm", "src")),
        P(("tm", "src")),
        P(("tm", "src")),
        P(("tm", "src")),
    )
    return jax.shard_map(
        on_device,
        mesh=mesh,
        in_specs=placed,
        out_specs=(P(None, ("tm", "src")), P()),
        check_vma=False,
    )
```

profile of v0, /device:TPU:0, one launch (start us, length us, event | category | flops | bytes accessed | tf_op | source)
XLA Modules:
  0.0 241.2 jit_solution(16647316104159535777)
XLA Ops:
  8.7 1.6 fusion.56
  10.3 42.7 %while.14 = (s32[]{:T(128)}, f32[272,128]{1,0:T(8,128)S(1)}, f32[16,16384]{1,0:T(8,128)}, f32[16384]{0:T(1024)S(1)}, f32[16384]{0:T(1024)}, /*index=5*/s32[16384...) while((s32[]{:T(128)}, f32[272,128]{1,0:T(8,128)S(1)}, f32[16,16384]{1,0:T(8,128)}, ...), condition=%wide.region_1.2_spmd.clone, body=%wide.region_0.1_spmd.clone.sunk | while | flops 428839936 | bytes 4837545 | solution.py:86
  54.9 90.6 %all-reduce.4.cloned.1.call-done = f32[272,128]{1,0:T(8,128)} async-done(((f32[272,128]{1,0:T(8,128)}), f32[272,128]{1,0:T(8,128)}) %all-reduce.4.cloned.1.call-update) | async-done | bytes 139280
  146.4 1.2 subtract_sqrt_fusion.8
  147.7 2.8 %subtract_divide_fusion.29 = (f32[8]{0:T(128)S(1)}, f32[8]{0:T(128)S(1)}, f32[8]{0:T(128)S(1)}, f32[8]{0:T(128)S(1)}, f32[8]{0:T(128)S(1)}, /*index=5*/f32[8]{0:...) fusion(f32[272,128]{1,0:T(8,128)} %all-reduce.4.cloned.1.call-d, ...), kind=kLoop, calls=%fused_computation.264 | loop fusion | flops 10472 | bytes 10624 | tf_op jit(solution)/shard_map/div | solution.py:33
  150.5 1.5 subtract_divide_fusion.15
  152.0 1.9 multiply_reduce_fusion
  154.6 1.4 fusion.9
  156.8 1.5 multiply_reduce_fusion.14
  158.2 1.4 multiply_reduce_fusion.15
  161.0 1.5 multiply_reduce_fusion.13
  163.2 1.5 multiply_reduce_fusion.12
  165.3 1.5 multiply_reduce_fusion.11
  167.5 1.5 multiply_reduce_fusion.10
  169.7 1.5 multiply_reduce_fusion.9
  171.8 1.5 multiply_reduce_fusion.8
  174.0 1.5 multiply_reduce_fusion.7
  176.2 1.5 multiply_reduce_fusion.6
  178.3 1.5 multiply_reduce_fusion.5
  180.5 1.5 multiply_reduce_fusion.4
  182.7 1.5 multiply_reduce_fusion.3
  184.8 1.5 multiply_reduce_fusion.2
  187.0 1.5 multiply_reduce_fusion.1
  190.5 41.3 %all-reduce.1 = (f32[]{:T(128)}, f32[]{:T(128)}) all-reduce(f32[]{:T(128)S(6)} %add.1126, f32[]{:T(128)} %get-tuple-element.154), channel_id=1, replica_groups=mesh['tm'=2,'src'=16] {'tm','src'}, use_global_device_ids=true, to_apply=%region_21.22 | all-reduce | flops 2 | bytes 16 | tf_op jit(solution)/shard_map/psum | solution.py:91
  (110 shorter events, 45.6 us)
Async XLA Ops:
  7.2 138.3 %all-reduce.4.cloned.1.call-start = ((), (), s32[]{:S(2)}) async-start(), calls=%async_computation | async-start | bytes 278528
  10.3 43.4 %copy-start.2 = (u32[32]{0:T(128)S(1)}, u32[32]{0:T(128)}, u32[]{:S(2)}) copy-start(u32[32]{0:T(128)} %constant.48) | copy-start | bytes 388
  10.3 135.2 %copy-start.1 = (f32[8]{0:T(128)S(1)}, f32[8]{0:T(128)}, u32[]{:S(2)}) copy-start(f32[8]{0:T(128)} %param.13) | copy-start | bytes 100
  53.0 0.7 copy-start
Sparse Core Ops, SparseCore 0:
  53.8 91.6 all-reduce.3
where the time goes:
time: 244 us; the launch traced here: 241 us
  waiting for transfers between devices  90.6 us (37%)
  other arithmetic  62.9 us (26%)
  blocking collectives  41.3 us (17%)
  between operations  30.2 us (12%)
  matrix products  13.1 us (5%)
    unnamed x2, waiting for transfers between devices  90.6 us
    psum x1, blocking collectives, on_device(): lax.psum((before + unit_terms, jnp.sum(weights_on)), ('tm', 'src'))  41.3 us
    reduce_sum x16, other arithmetic, quadratic_terms(): quadratic = quadratic + jnp.sum(solution_own[i] * applied)  24 us
    mul x16, other arithmetic, accumulate(): rows * (weights_blk * resid)  13.6 us
    dot_general x16, matrix products, accumulate(): jnp.dot(stacked, one_hot, precision=lax.Precision.HIGHEST, preferred_elem...  13.1 us
    mul x16, other arithmetic, accumulate(): weights_blk * resid  11.1 us
  transfers between devices with their start and end apart: 1, of which 1 were waited for; matrix products, arithmetic and copies ran while one was open for 0% of the time, Pallas kernels for 0%

commit v1 on v0

v1 whole, which is shorter than its diff:
```python
import functools

import jax
import jax.numpy as jnp
from jax import lax
from jax.experimental import pallas as pl
from jax.experimental.pallas import tpu as pltpu
from jax.sharding import PartitionSpec as P

WIDTH = 16
HALF = 8
PAIRS = WIDTH * (WIDTH + 1) // 2
ROWS = PAIRS + WIDTH
LANES = 128
ROWS_PAD = 256


def pair_row(i, j):
    k = (j - i) % WIDTH
    if k > HALF or (k == HALF and i >= HALF):
        i, j = j, i
        k = (j - i) % WIDTH
    return k * WIDTH + i


def stacked_rows(d0, d1, w, wr):
    w0, w1 = d0 * w, d1 * w
    rows = [d0 * w0, d1 * w1]
    sub = lax.broadcasted_iota(jnp.int32, d0.shape, 0)
    for k in range(1, HALF):
        r0 = pltpu.roll(w0, HALF - k, 0)
        r1 = pltpu.roll(w1, HALF - k, 0)
        low = sub < HALF - k
        rows.append(d0 * jnp.where(low, r0, r1))
        rows.append(d1 * jnp.where(low, r1, r0))
    rows.append(d0 * w1)
    rows.append(d0 * wr)
    rows.append(d1 * wr)
    return rows


def rsqrt(value):
    guess = lax.rsqrt(value)
    return guess * (1.5 - 0.5 * value * guess * guess)


def solve(entry, rhs, damping):
    a = {}
    for i in range(WIDTH):
        for j in range(i + 1):
            a[i, j] = entry(i, j)
        a[i, i] = a[i, i] + damping
    b = [rhs(i) for i in range(WIDTH)]
    inverse, forward = [], []
    for j in range(WIDTH):
        inv = rsqrt(a[j, j])
        inverse.append(inv)
        for i in range(j + 1, WIDTH):
            a[i, j] = a[i, j] * inv
        y = b[j] * inv
        forward.append(y)
        for i in range(j + 1, WIDTH):
            b[i] = b[i] - a[i, j] * y
            for k in range(j + 1, i + 1):
                a[i, k] = a[i, k] - a[i, j] * a[k, j]
    run = list(forward)
    x = [None] * WIDTH
    for i in reversed(range(WIDTH)):
        x[i] = run[i] * inverse[i]
        for k in range(i):
            run[k] = run[k] - a[i, k] * x[i]
    return x, forward


def kernel(
    n_tm, n_src, chunk,
    count_ref, design_ref, unit_ref, resid_ref, weight_ref, damp_ref,
    x_ref, misfit_ref,
    acc, part, got, summed, mine, heard,
    send_a, recv_a, send_b, recv_b,
):
    tm, src = lax.axis_index("tm"), lax.axis_index("src")
    n_all = n_tm * n_src
    me = tm * n_src + src
    own = damp_ref.shape[1]
    units = own * n_src
    slots = design_ref.shape[1]

    def place(flat):
        return {"tm": flat // n_src, "src": flat % n_src}

    barrier = pltpu.get_barrier_semaphore()

    def greet(p, c):
        pl.semaphore_signal(
            barrier, inc=1, device_id=place((me + p) % n_all), device_id_type=pl.DeviceIdType.MESH
        )
        return c

    lax.fori_loop(1, n_all, greet, 0)

    count = count_ref[0]
    first_unit = tm * units
    acc[...] = jnp.zeros_like(acc)

    def accumulate(step, carry):
        chi, total = carry
        begin = pl.multiple_of(step * chunk, chunk)
        cols = pl.ds(begin, chunk)
        w = weight_ref[:, cols]
        live = begin + lax.broadcasted_iota(jnp.int32, w.shape, 1) < count
        w = jnp.where(live, w, 0.0)
        r = resid_ref[:, cols]
        wr = w * r
        rows = stacked_rows(design_ref[0:HALF, cols], design_ref[HALF:WIDTH, cols], w, wr)
        x = jnp.concatenate(rows, axis=0)
        high = x.astype(jnp.bfloat16).astype(jnp.float32)
        lhs = jnp.concatenate([high, x - high], axis=0).astype(jnp.bfloat16)
        unit = unit_ref[:, cols] - first_unit
        hot = lax.broadcasted_iota(jnp.int32, (units, chunk), 0) == unit
        hot = jnp.where(hot, 1.0, 0.0).astype(jnp.bfloat16)
        acc[...] += lax.dot_general(
            lhs, hot, (((1,), (1,)), ((), ())), preferred_element_type=jnp.float32
        )
        wrr = wr * r
        for t in range(chunk // LANES):
            chi = chi + wrr[:, t * LANES:(t + 1) * LANES]
            total = total + w[:, t * LANES:(t + 1) * LANES]
        return chi, total

    zero = jnp.zeros((1, LANES), jnp.float32)
    chi, total = lax.fori_loop(0, slots // chunk, accumulate, (zero, zero))

    sums = acc[0:ROWS] + acc[ROWS:2 * ROWS]
    sums = jnp.concatenate([sums, jnp.zeros((ROWS_PAD - ROWS, units), jnp.float32)], axis=0)
    part[...] = jnp.transpose(sums).reshape(n_src, own, ROWS_PAD)

    pl.semaphore_wait(barrier, n_all - 1)

    def exchange(p):
        to = (src + p) % n_src
        return pltpu.make_async_remote_copy(
            src_ref=part.at[to], dst_ref=got.at[src],
            send_sem=send_a.at[to], recv_sem=recv_a.at[src],
            device_id={"tm": tm, "src": to}, device_id_type=pl.DeviceIdType.MESH,
        )

    def arrival(p):
        frm = (src + p) % n_src
        return frm, pltpu.make_async_remote_copy(
            src_ref=part.at[frm], dst_ref=got.at[frm],
            send_sem=send_a.at[frm], recv_sem=recv_a.at[frm],
            device_id={"tm": tm, "src": frm}, device_id_type=pl.DeviceIdType.MESH,
        )

    def send_one(p, c):
        exchange(p).start()
        return c

    lax.fori_loop(1, n_src, send_one, 0)

    def take_one(p, value):
        frm, copy = arrival(p)
        copy.wait_recv()
        return value + got[frm]

    whole = lax.fori_loop(1, n_src, take_one, part[src])
    summed[...] = jnp.transpose(whole)

    damping = damp_ref[...]
    x, forward = solve(
        lambda i, j: summed[pl.ds(pair_row(i, j), 1), :],
        lambda i: summed[pl.ds(PAIRS + i, 1), :],
        damping,
    )
    terms = jnp.zeros_like(damping)
    squared = jnp.zeros_like(damping)
    for i in range(WIDTH):
        x_ref[i:i + 1, :] = x[i]
        terms = terms + forward[i] * forward[i]
        squared = squared + x[i] * x[i]
    terms = terms + damping * squared
    chi = chi - jnp.concatenate([terms, jnp.zeros((1, LANES - own), jnp.float32)], axis=1)
    lane = lax.broadcasted_iota(jnp.int32, (1, LANES), 1)
    front = lane < LANES // 2
    chi = chi + pltpu.roll(chi, LANES // 2, 1)
    total = total + pltpu.roll(total, LANES // 2, 1)
    mine[...] = jnp.where(front, chi, total)

    def tell(p, c):
        to = (me + p) % n_all
        pltpu.make_async_remote_copy(
            src_ref=mine, dst_ref=heard.at[me],
            send_sem=send_b.at[to], recv_sem=recv_b.at[me],
            device_id=place(to), device_id_type=pl.DeviceIdType.MESH,
        ).start()
        return c

    lax.fori_loop(1, n_all, tell, 0)

    def hear(p, value):
        frm = (me + p) % n_all
        copy = pltpu.make_async_remote_copy(
            src_ref=mine, dst_ref=heard.at[frm],
            send_sem=send_b.at[frm], recv_sem=recv_b.at[frm],
            device_id=place(frm), device_id_type=pl.DeviceIdType.MESH,
        )
        copy.wait_recv()
        return value + heard[frm]

    both = lax.fori_loop(1, n_all, hear, mine[...])
    chi_all = jnp.sum(jnp.where(front, both, 0.0), axis=1, keepdims=True)
    total_all = jnp.sum(jnp.where(front, 0.0, both), axis=1, keepdims=True)
    misfit_ref[...] = chi_all / total_all

    def drain_a(p, c):
        exchange(p).wait_send()
        return c

    lax.fori_loop(1, n_src, drain_a, 0)

    def drain_b(p, c):
        to = (me + p) % n_all
        pltpu.make_async_remote_copy(
            src_ref=mine, dst_ref=heard.at[me],
            send_sem=send_b.at[to], recv_sem=recv_b.at[me],
            device_id=place(to), device_id_type=pl.DeviceIdType.MESH,
        ).wait_send()
        return c

    lax.fori_loop(1, n_all, drain_b, 0)


def solution(mesh):
    n_tm, n_src = mesh.shape["tm"], mesh.shape["src"]
    n_all = n_tm * n_src

    def on_device(design, unit_index, residual, weight, obs_count, damping):
        own = damping.shape[0]
        units = own * n_src
        slots = design.shape[1]
        chunk = 2048 if slots % 2048 == 0 else LANES
        vmem = pl.BlockSpec(memory_space=pltpu.VMEM)
        x, misfit = pl.pallas_call(
            functools.partial(kernel, n_tm, n_src, chunk),
            out_shape=(
                jax.ShapeDtypeStruct((WIDTH, own), jnp.float32),
                jax.ShapeDtypeStruct((1, 1), jnp.float32),
            ),
            in_specs=[pl.BlockSpec(memory_space=pltpu.SMEM)] + [vmem] * 5,
            out_specs=(vmem, vmem),
            scratch_shapes=[
                pltpu.VMEM((2 * ROWS, units), jnp.float32),
                pltpu.VMEM((n_src, own, ROWS_PAD), jnp.float32),
                pltpu.VMEM((n_src, own, ROWS_PAD), jnp.float32),
                pltpu.VMEM((ROWS_PAD, own), jnp.float32),
                pltpu.VMEM((1, LANES), jnp.float32),
                pltpu.VMEM((n_all, 1, LANES), jnp.float32),
                pltpu.SemaphoreType.DMA((n_src,)),
                pltpu.SemaphoreType.DMA((n_src,)),
                pltpu.SemaphoreType.DMA((n_all,)),
                pltpu.SemaphoreType.DMA((n_all,)),
            ],
            compiler_params=pltpu.CompilerParams(collective_id=0, has_side_effects=True),
            name="calibrate",
        )(
            obs_count,
            design,
            unit_index.reshape(1, slots),
            residual.reshape(1, slots),
            weight.reshape(1, slots),
            damping.reshape(1, own),
        )
        return x, misfit.reshape(())

    both = ("tm", "src")
    return jax.shard_map(
        on_device,
        mesh=mesh,
        in_specs=(P(None, both), P(both), P(both), P(both), P(both), P(both)),
        out_specs=(P(None, both), P()),
        check_vma=False,
    )
```

time: 244 us -> 25.9 us (0.11); the launches traced: 241 us -> 25.6 us
  waiting for transfers between devices: 90.6 us -> 0 us
  other arithmetic: 62.9 us -> 0 us
  blocking collectives: 41.3 us -> 0 us
  between operations: 30.2 us -> 3.05 us
  Pallas kernels: 0 us -> 21.2 us
  matrix products: 13.1 us -> 0 us
    unnamed x2 -> x0, waiting for transfers between devices: 90.6 us -> none
    psum x1 -> x0, blocking collectives: 41.3 us -> none  [on_device(): lax.psum((before + unit_terms, jnp.sum(weights_on)), ('tm', 'src'))]
    mul x64 -> x0, other arithmetic: 28.5 us -> none  [the longest x16 13.6 us: accumulate(): rows * (weights_blk * resid)]
    reduce_sum x18 -> x0, other arithmetic: 27.1 us -> none  [the longest x16 24 us: quadratic_terms(): quadratic = quadratic + jnp.sum(solution_own[i] * applied)]
    pallas_call x0 -> x1, Pallas kernels: none -> 21.2 us  [on_device(): pl.pallas_call(functools.partial(kernel, n_tm, n_src, chunk), out_shape=(...]
    dot_general x16 -> x0, matrix products: 13.1 us -> none  [accumulate(): jnp.dot(stacked, one_hot, precision=lax.Precision.HIGHEST, preferred_elem...]
    div x3 -> x0, other arithmetic: 5.25 us -> none  [the longest x1 2.78 us: block_solve(): forward.append(running / lower[i, i])]
  transfers between devices with their start and end apart: 1 -> 0, of which waited for: 1 -> 0; matrix products, arithmetic and copies ran while one was open for 0% -> 0% of each run, Pallas kernels for 0% -> 0%
where the time goes in v1:
time: 25.9 us; the launch traced here: 25.6 us
  Pallas kernels  21.2 us (82%)
  between operations  3.05 us (12%)
  local copies, waits for them, and re-layouts  1.36 us (5%)
    pallas_call x1, Pallas kernels, on_device(): pl.pallas_call(functools.partial(kernel, n_tm, n_src, chunk), out_shape=(...  21.2 us
    unnamed x1, local copies, waits for them, and re-layouts  1.36 us

profile of v1, /device:TPU:0, one launch (start us, length us, event | category | flops | bytes accessed | tf_op | source)
XLA Modules:
  0.0 25.6 jit_solution(3685270028317910535)
XLA Ops:
  1.3 21.2 %calibrate.1 = (f32[16,8]{1,0:T(8,128)}, f32[1,1]{1,0:T(1,128)}) custom-call(s32[1]{0:T(128)S(6)} %copy.10.count_ref, f32[16,16384]{1,0:T(8,128)} %design_ref.1, s32[1,16384]{1,0:T(1,128)} %bitcast.5, f32[1,16384]{1,0:T(1,128)} %bitcast.6, f32[1,16384]{1,0:T(1,128)} %bitcast.7, f32[1,8]{1,0:T(1,128)} %bitcast.8), custom_call_target="tpu_custom_call" | custom-call | tf_op jit(solution)/shard_map/calibrate/pallas_call | solution.py:244
  22.5 1.4 %copy.8 = f32[16,8]{0,1:T(8,128)} copy(f32[16,8]{1,0:T(8,128)} %get-tuple-element.6) | data formatting | bytes 1024

commit v2 on v1

v2 whole, which is shorter than its diff:
```python
import functools

import jax
import jax.numpy as jnp
from jax import lax
from jax.experimental import pallas as pl
from jax.experimental.pallas import tpu as pltpu
from jax.sharding import PartitionSpec as P

WIDTH = 16
HALF = 8
PAIRS = WIDTH * (WIDTH + 1) // 2
ROWS = PAIRS + WIDTH
LANES = 128
FOLD = 4


def pair_row(i, j):
    k = (j - i) % WIDTH
    if k > HALF or (k == HALF and i >= HALF):
        i, j = j, i
        k = (j - i) % WIDTH
    return k * WIDTH + i


def stacked_rows(d0, d1, w, wr):
    w0, w1 = d0 * w, d1 * w
    rows = [d0 * w0, d1 * w1]
    sub = lax.broadcasted_iota(jnp.int32, d0.shape, 0)
    for k in range(1, HALF):
        r0 = pltpu.roll(w0, HALF - k, 0)
        r1 = pltpu.roll(w1, HALF - k, 0)
        low = sub < HALF - k
        rows.append(d0 * jnp.where(low, r0, r1))
        rows.append(d1 * jnp.where(low, r1, r0))
    rows.append(d0 * w1)
    rows.append(d0 * wr)
    rows.append(d1 * wr)
    return rows


def rsqrt(value):
    guess = lax.rsqrt(value)
    return guess * (1.5 - 0.5 * value * guess * guess)


def solve(entry, rhs, damping):
    a = {}
    for i in range(WIDTH):
        for j in range(i + 1):
            a[i, j] = entry(i, j)
        a[i, i] = a[i, i] + damping
    b = [rhs(i) for i in range(WIDTH)]
    inverse, forward = [], []
    for j in range(WIDTH):
        inv = rsqrt(a[j, j])
        inverse.append(inv)
        for i in range(j + 1, WIDTH):
            a[i, j] = a[i, j] * inv
        y = b[j] * inv
        forward.append(y)
        for i in range(j + 1, WIDTH):
            b[i] = b[i] - a[i, j] * y
            for k in range(j + 1, i + 1):
                a[i, k] = a[i, k] - a[i, j] * a[k, j]
    run = list(forward)
    x = [None] * WIDTH
    for i in reversed(range(WIDTH)):
        x[i] = run[i] * inverse[i]
        for k in range(i):
            run[k] = run[k] - a[i, k] * x[i]
    return x, forward


def far_first(n):
    q = max(n // 4, 1)
    order = []
    for i in range(q):
        order += [3 * q + i, q + i]
    order += list(range(2 * q, 3 * q)) + list(range(1, q))
    return [p for p in dict.fromkeys(order) if 0 < p < n]


def each(pairs, body, start):
    if len(pairs) <= 32:
        for dt, dp in pairs:
            start = body(dt, dp, start)
        return start
    n_src = max(dp for _, dp in pairs) + 1
    return lax.fori_loop(
        1, len(pairs) + 1, lambda i, c: body(i // n_src, i % n_src, c), start
    )


def kernel(
    n_tm, n_src, chunk,
    count_hbm, design_hbm, unit_hbm, resid_hbm, weight_hbm, damp_hbm,
    x_ref, misfit_ref,
    count_ref, design_ref, unit_ref, resid_ref, weight_ref, damp_ref,
    acc, extra, part, tail, got, got_tail, summed, spread, mine, heard,
    load, small, send_a, recv_a, send_b, recv_b,
):
    tm, src = lax.axis_index("tm"), lax.axis_index("src")
    n_all = n_tm * n_src
    me = tm * n_src + src
    own = damp_ref.shape[1]
    units = own * n_src
    slots = design_ref.shape[1]
    turns = slots // chunk
    order = far_first(n_src)
    near = [(0, p) for p in order]
    everyone = [(dt, p) for dt in range(n_tm - 1, 0, -1) for p in order + [0]] + near

    arrays = (
        (design_hbm, design_ref), (unit_hbm, unit_ref),
        (resid_hbm, resid_ref), (weight_hbm, weight_ref),
    )

    def fetch(step, which):
        far, here = arrays[which]
        cols = pl.ds(pl.multiple_of(step * chunk, chunk), chunk)
        return pltpu.make_async_copy(far.at[:, cols], here.at[:, cols], load.at[step, which])

    count_copy = pltpu.make_async_copy(count_hbm, count_ref, small.at[0])
    damp_copy = pltpu.make_async_copy(damp_hbm, damp_ref, small.at[1])
    count_copy.start()
    for which in range(4):
        fetch(0, which).start()
    for step in range(1, turns):
        for which in range(4):
            fetch(step, which).start()
    damp_copy.start()

    def at(dt, dp):
        return {"tm": (tm + dt) % n_tm, "src": (src + dp) % n_src}

    barrier = pltpu.get_barrier_semaphore()

    def greet(dt, dp, c):
        pl.semaphore_signal(
            barrier, inc=1, device_id=at(dt, dp), device_id_type=pl.DeviceIdType.MESH
        )
        return c

    each(everyone, greet, 0)

    first_unit = tm * units
    zero = jnp.zeros((1, LANES), jnp.float32)
    count_copy.wait()
    count = count_ref[0]

    def accumulate(step, carry):
        chi, total = carry
        for which in range(4):
            fetch(step, which).wait()
        begin = pl.multiple_of(step * chunk, chunk)
        cols = pl.ds(begin, chunk)
        w = weight_ref[:, cols]
        live = begin + lax.broadcasted_iota(jnp.int32, w.shape, 1) < count
        w = jnp.where(live, w, 0.0)
        r = resid_ref[:, cols]
        wr = w * r
        rows = stacked_rows(design_ref[0:HALF, cols], design_ref[HALF:WIDTH, cols], w, wr)
        x = jnp.concatenate(rows, axis=0)
        high = x.astype(jnp.bfloat16).astype(jnp.float32)
        lhs = jnp.concatenate([high, x - high], axis=0).astype(jnp.bfloat16)
        unit = unit_ref[:, cols] - first_unit
        hot = lax.broadcasted_iota(jnp.int32, (units, chunk), 0) == unit
        hot = jnp.where(hot, 1.0, 0.0).astype(jnp.bfloat16)
        acc[...] += lax.dot_general(
            lhs, hot, (((1,), (1,)), ((), ())), preferred_element_type=jnp.float32
        )
        wrr = wr * r
        for t in range(chunk // LANES):
            chi = chi + wrr[:, t * LANES:(t + 1) * LANES]
            total = total + w[:, t * LANES:(t + 1) * LANES]
        return chi, total

    acc[...] = jnp.zeros_like(acc)
    chi, total = lax.fori_loop(0, turns, accumulate, (zero, zero))

    sums = acc[0:ROWS] + acc[ROWS:2 * ROWS]
    left = jnp.concatenate(
        [sums[LANES:ROWS], jnp.zeros((2 * LANES - ROWS, units), jnp.float32)], axis=0
    )
    extra[...] = jnp.transpose(left)
    part[...] = jnp.transpose(sums[0:LANES]).reshape(n_src, own, LANES)
    packed = extra[pl.ds(0, units // FOLD, stride=FOLD), :]
    for b in range(1, FOLD):
        packed = packed + pltpu.roll(
            extra[pl.ds(b, units // FOLD, stride=FOLD), :], b * (LANES // FOLD), 1
        )
    tail[...] = packed.reshape(n_src, own // FOLD, LANES)

    pl.semaphore_wait(barrier, n_all - 1)

    def exchange(peer, slot, which):
        mine_of, theirs = ((part, got), (tail, got_tail))[which]
        return pltpu.make_async_remote_copy(
            src_ref=mine_of.at[peer], dst_ref=theirs.at[slot],
            send_sem=send_a.at[which, peer], recv_sem=recv_a.at[which, slot],
            device_id={"tm": tm, "src": peer}, device_id_type=pl.DeviceIdType.MESH,
        )

    def send_one(dt, dp, c):
        to = (src + dp) % n_src
        exchange(to, src, 0).start()
        exchange(to, src, 1).start()
        return c

    each(near, send_one, 0)

    def take_one(dt, dp, carry):
        frm = (src - dp + n_src) % n_src
        exchange(frm, frm, 0).wait_recv()
        exchange(frm, frm, 1).wait_recv()
        return carry[0] + got[frm], carry[1] + got_tail[frm]

    whole, ends = each(list(reversed(near)), take_one, (part[src], tail[src]))
    for a in range(own // FOLD):
        for b in range(FOLD):
            row = ends[a:a + 1]
            spread[pl.ds(a * FOLD + b, 1), :] = (
                pltpu.roll(row, LANES - b * (LANES // FOLD), 1) if b else row
            )
    summed[0:LANES, :] = jnp.transpose(whole)
    summed[LANES:2 * LANES, :] = jnp.transpose(spread[...])

    damp_copy.wait()
    damping = damp_ref[...]
    x, forward = solve(
        lambda i, j: summed[pl.ds(pair_row(i, j), 1), :],
        lambda i: summed[pl.ds(PAIRS + i, 1), :],
        damping,
    )
    terms = jnp.zeros_like(damping)
    squared = jnp.zeros_like(damping)
    for i in range(WIDTH):
        terms = terms + forward[i] * forward[i]
        squared = squared + x[i] * x[i]
    terms = terms + damping * squared
    chi = chi - jnp.concatenate([terms, jnp.zeros((1, LANES - own), jnp.float32)], axis=1)
    lane = lax.broadcasted_iota(jnp.int32, (1, LANES), 1)
    front = lane < LANES // 2
    chi = chi + pltpu.roll(chi, LANES // 2, 1)
    total = total + pltpu.roll(total, LANES // 2, 1)
    mine[...] = jnp.where(front, chi, total)

    def tell(dt, dp):
        to = ((tm + dt) % n_tm) * n_src + (src + dp) % n_src
        return pltpu.make_async_remote_copy(
            src_ref=mine, dst_ref=heard.at[me],
            send_sem=send_b.at[to], recv_sem=recv_b.at[me],
            device_id=at(dt, dp), device_id_type=pl.DeviceIdType.MESH,
        )

    def tell_one(dt, dp, c):
        tell(dt, dp).start()
        return c

    each(everyone, tell_one, 0)

    x_ref[...] = jnp.transpose(jnp.concatenate(x, axis=0))

    def hear_one(dt, dp, value):
        frm = ((tm + dt) % n_tm) * n_src + (src + dp) % n_src
        pltpu.make_async_remote_copy(
            src_ref=mine, dst_ref=heard.at[frm],
            send_sem=send_b.at[frm], recv_sem=recv_b.at[frm],
            device_id=at(dt, dp), device_id_type=pl.DeviceIdType.MESH,
        ).wait_recv()
        return value + heard[frm]

    def drain_a(dt, dp, c):
        to = (src + dp) % n_src
        exchange(to, src, 0).wait_send()
        exchange(to, src, 1).wait_send()
        return c

    each(near, drain_a, 0)
    both = each(list(reversed(everyone)), hear_one, mine[...])
    chi_all = jnp.sum(jnp.where(front, both, 0.0), axis=1, keepdims=True)
    total_all = jnp.sum(jnp.where(front, 0.0, both), axis=1, keepdims=True)
    misfit_ref[...] = chi_all / total_all

    def drain_b(dt, dp, c):
        tell(dt, dp).wait_send()
        return c

    each(everyone, drain_b, 0)


def hand_on(x_ref, misfit_ref, x_out, misfit_out):
    x_out[...] = x_ref[...]
    misfit_out[...] = misfit_ref[...]


def solution(mesh):
    n_tm, n_src = mesh.shape["tm"], mesh.shape["src"]
    n_all = n_tm * n_src

    def on_device(design, unit_index, residual, weight, obs_count, damping):
        own = damping.shape[0]
        units = own * n_src
        slots = design.shape[1]
        chunk = 8192 if slots % 8192 == 0 else LANES
        turns = slots // chunk
        anywhere = pl.BlockSpec(memory_space=pl.ANY)
        vmem = pl.BlockSpec(memory_space=pltpu.VMEM)
        x, misfit = pl.pallas_call(
            functools.partial(kernel, n_tm, n_src, chunk),
            out_shape=(
                jax.ShapeDtypeStruct((own, WIDTH), jnp.float32),
                jax.ShapeDtypeStruct((1, 1), jnp.float32),
            ),
            in_specs=[anywhere] * 6,
            out_specs=(vmem, vmem),
            scratch_shapes=[
                pltpu.SMEM((1,), jnp.int32),
                pltpu.VMEM((WIDTH, slots), jnp.float32),
                pltpu.VMEM((1, slots), jnp.int32),
                pltpu.VMEM((1, slots), jnp.float32),
                pltpu.VMEM((1, slots), jnp.float32),
                pltpu.VMEM((1, own), jnp.float32),
                pltpu.VMEM((2 * ROWS, units), jnp.float32),
                pltpu.VMEM((units, LANES), jnp.float32),
                pltpu.VMEM((n_src, own, LANES), jnp.float32),
                pltpu.VMEM((n_src, own // FOLD, LANES), jnp.float32),
                pltpu.VMEM((n_src, own, LANES), jnp.float32),
                pltpu.VMEM((n_src, own // FOLD, LANES), jnp.float32),
                pltpu.VMEM((2 * LANES, own), jnp.float32),
                pltpu.VMEM((own, LANES), jnp.float32),
                pltpu.VMEM((1, LANES), jnp.float32),
                pltpu.VMEM((n_all, 1, LANES), jnp.float32),
                pltpu.SemaphoreType.DMA((turns, 4)),
                pltpu.SemaphoreType.DMA((2,)),
                pltpu.SemaphoreType.DMA((2, n_src)),
                pltpu.SemaphoreType.DMA((2, n_src)),
                pltpu.SemaphoreType.DMA((n_all,)),
                pltpu.SemaphoreType.DMA((n_all,)),
            ],
            compiler_params=pltpu.CompilerParams(collective_id=0, has_side_effects=True),
            name="calibrate",
        )(
            obs_count,
            design,
            unit_index.reshape(1, slots),
            residual.reshape(1, slots),
            weight.reshape(1, slots),
            damping.reshape(1, own),
        )
        x, misfit = pl.pallas_call(
            hand_on,
            out_shape=(
                jax.ShapeDtypeStruct((own, WIDTH), jnp.float32),
                jax.ShapeDtypeStruct((1, 1), jnp.float32),
            ),
            in_specs=[vmem, vmem],
            out_specs=(vmem, vmem),
            name="hand_on",
        )(x, misfit)
        return x.T, misfit.reshape(())

    both = ("tm", "src")
    return jax.shard_map(
        on_device,
        mesh=mesh,
        in_specs=(P(None, both), P(both), P(both), P(both), P(both), P(both)),
        out_specs=(P(None, both), P()),
        check_vma=False,
    )
```

time: 25.9 us -> 22.1 us (0.85)
  between operations: 3.05 us -> 1.29 us
  local copies, waits for them, and re-layouts: 1.36 us -> 0 us
  Pallas kernels: 21.2 us -> 20.6 us
    pallas_call x1, Pallas kernels: 21.2 us -> 18.7 us  [on_device(): pl.pallas_call(functools.partial(kernel, n_tm, n_src, chunk), out_shape=(...]
    pallas_call x0 -> x1, Pallas kernels: none -> 1.9 us  [on_device(): pl.pallas_call(hand_on, out_shape=(jax.ShapeDtypeStruct((own, WIDTH), jnp...]
    unnamed x1 -> x0, local copies, waits for them, and re-layouts: 1.36 us -> none
where the time goes in v2:
time: 22.1 us; the launch traced here: 21.9 us
  Pallas kernels  20.6 us (93%)
  between operations  1.29 us (6%)
    pallas_call x1, Pallas kernels, on_device(): pl.pallas_call(functools.partial(kernel, n_tm, n_src, chunk), out_shape=(...  18.7 us
    pallas_call x1, Pallas kernels, on_device(): pl.pallas_call(hand_on, out_shape=(jax.ShapeDtypeStruct((own, WIDTH), jnp...  1.9 us

profile of v2, /device:TPU:0, one launch (start us, length us, event | category | flops | bytes accessed | tf_op | source)
XLA Modules:
  0.0 21.9 jit_solution(12541056939466410961)
XLA Ops:
  1.3 18.7 %calibrate.1 = (f32[8,16]{1,0:T(8,128)}, f32[1,1]{1,0:T(1,128)}) custom-call(s32[1]{0:T(128)S(6)} %copy.8.count_hbm, f32[16,16384]{1,0:T(8,128)} %design_hbm.1, s32[1,16384]{1,0:T(1,128)} %bitcast.6, f32[1,16384]{1,0:T(1,128)} %bitcast.7, f32[1,16384]{1,0:T(1,128)} %bitcast.8, f32[1,8]{1,0:T(1,128)} %bitcast.9), custom_call_target="tpu_custom_call" | custom-call | tf_op jit(solution)/shard_map/calibrate/pallas_call | solution.py:310
  20.0 1.9 %hand_on.1 = (f32[8,16]{1,0:T(8,128)}, f32[1,1]{1,0:T(1,128)}) custom-call(f32[8,16]{1,0:T(8,128)} %get-tuple-element.6.x_ref, f32[1,1]{1,0:T(1,128)} %get-tuple-element.7.misfit_ref), custom_call_target="tpu_custom_call" | custom-call | tf_op jit(solution)/shard_map/hand_on/pallas_call | solution.py:352
